TPU v7x, 256 devices: a whole 4x4x8 slice. The times are simulated.
256 devices in a mesh: row: 8 (over z), col: 8 (over y, core), depth: 4 (over x).
Axes of the slice: x: 4, y: 4, z: 8, core: 2. Of those that a mesh axis runs over, the one named last changes fastest.
Arguments:
- a21_leaf: float32 [4, 4096, 2048], P('depth', 'row', 'col'), may hold values from -1.2 to 1.2
- a12_leaf: float32 [4, 2048, 4096], P('depth', 'row', 'col'), may hold values from -1.2 to 1.2
- uinv_leaf: float32 [4, 2048, 2048], P('depth', None, 'col'), may hold values from -0.2 to 1.5, as said below
- linv_leaf: float32 [4, 2048, 2048], P('depth', 'row'), may hold values from -0.2 to 1.5, as said below
- live: int32 [4], P('depth'), may hold values from 16 to 32
- row_map: int32 [4, 32], P('depth', 'row'), may hold values from 0 to 63, as said below
- col_map: int32 [4, 32], P('depth', 'col'), may hold values from 0 to 63, as said below
- a22_anc: float32 [8192, 8192], P(('row', 'depth'), 'col'), may hold values from -6 to 6
- a21_anc: float32 [8192, 2048], P(('row', 'depth'), 'col'), may hold values from -1.2 to 1.2
- a12_anc: float32 [2048, 8192], P(('row', 'depth'), 'col'), may hold values from -1.2 to 1.2
- uinv_anc: float32 [2048, 2048], P(None, 'col'), may hold values from -0.2 to 1.5, as said below
- linv_anc: float32 [2048, 2048], P(('row', 'depth')), may hold values from -0.2 to 1.5, as said below
Outputs:
- leaf_lower: float32 [4, 4096, 2048], P('depth', 'row', 'col')
- leaf_upper: float32 [4, 2048, 4096], P('depth', 'row', 'col')
- anc_lower: float32 [8192, 2048], P(('row', 'depth'), 'col')
- anc_upper: float32 [2048, 8192], P(('row', 'depth'), 'col')
- anc_schur: float32 [8192, 8192], P(('row', 'depth'), 'col')
Inputs may be any that keep to these rules, and one draw needn't show every extreme that they name: `uinv_leaf`: upper triangular: zero below the diagonal, diagonal between 0.5 and 1.5. `linv_leaf`: lower triangular: zero above the diagonal, diagonal between 0.5 and 1.5. `uinv_anc`: upper triangular: zero below the diagonal, diagonal between 0.5 and 1.5. `linv_anc`: lower triangular: zero above the diagonal, diagonal between 0.5 and 1.5. `row_map`: within one replica the entries are distinct. Leaf block row i lies in the k-th of 8 equal ranges of leaf block rows, and its target lies in the k-th of 8 equal ranges of the 64 ancestor block rows. `col_map`: within one replica the entries are distinct. Leaf block column j lies in the k-th of 8 equal ranges of leaf block columns, and its target lies in the k-th of 8 equal ranges of the 64 ancestor block columns.
All inputs are finite; a program needn't handle non-finite values.
Results may differ from a plain program's by a relative error of at most 0.0001.
Values sent between devices are 32-bit elements; how exact they have to be, the bound alone decides.
No kernel may reach another device: no remote copies, remote signals or barrier semaphores. Data moves between devices by JAX's collectives and lax.ppermute only.
A program may use at most 128 MiB of HBM per device.

v0:
```python
import math
import jax
import jax.numpy as jnp
from jax import lax
from jax.sharding import PartitionSpec as P

NB = 128


def in_one_piece(arrays, axis, split_dim, concat_dim, along):
    widths = [math.prod(a.shape[along:]) for a in arrays]
    both = jnp.concatenate(
        [a.reshape(*a.shape[:along], w) for a, w in zip(arrays, widths)], axis=along
    )
    out = lax.all_to_all(both, axis, split_axis=split_dim, concat_axis=concat_dim, tiled=True)
    tiles = jnp.split(out, [sum(widths[:k]) for k in range(1, len(widths))], axis=along)
    return tuple((b.reshape(*out.shape[:along], *a.shape[along:]) for a, b in zip(arrays, tiles)))


def sent_to_all(shard, axis):
    copies = jnp.broadcast_to(shard, (lax.axis_size(axis), *shard.shape))
    return lax.all_to_all(copies, axis, split_axis=0, concat_axis=0, tiled=True)


def in_order(tiles, dim):
    lengths = list(tiles.shape[1:])
    lengths[dim] *= tiles.shape[0]
    return jnp.moveaxis(tiles, 0, dim).reshape(lengths)


def collect(shard, axis, dim):
    tiles = sent_to_all(shard, axis)
    return in_order(tiles, dim)


def gather_axes(shard, axes, dim):
    out = shard
    for number in range(len(axes) - 1, -1, -1):
        out = lax.all_gather(out, axes[number], axis=dim, tiled=True)
    return out


def product(left, right):
    return jnp.dot(left, right, precision=lax.Precision.HIGHEST, preferred_element_type=jnp.float32)


def combine_depth(schur, row_map, col_map, a22_anc):
    block_size = NB
    rows_here = schur.shape[0]
    cols_here = schur.shape[1]
    leaf_rows = rows_here // block_size
    leaf_cols = cols_here // block_size
    anc_rows = a22_anc.shape[0]
    replicas = lax.axis_size("depth")
    anc_row_blocks = anc_rows * replicas // block_size
    anc_col_blocks = a22_anc.shape[1] // block_size
    row_local = row_map[0] - lax.axis_index("row") * anc_row_blocks
    col_local = col_map[0] - lax.axis_index("col") * anc_col_blocks
    owner_blocks = anc_rows // block_size
    slots = min(leaf_rows, owner_blocks)
    owner = row_local // owner_blocks
    earlier = lax.iota(jnp.int32, leaf_rows)[:, None] > lax.iota(jnp.int32, leaf_rows)[None, :]
    same = owner[:, None] == owner[None, :]
    rank = jnp.sum((earlier & same).astype(jnp.int32), axis=1)
    select = (
        (owner[:, None, None] == lax.iota(jnp.int32, replicas)[None, :, None])
        & (rank[:, None, None] == lax.iota(jnp.int32, slots)[None, None, :])
    ).astype(jnp.float32)
    leaf_blocks = schur.reshape(leaf_rows, block_size, cols_here)
    packed = jnp.einsum("iqs,ixc->qsxc", select, leaf_blocks, precision=lax.Precision.HIGHEST)
    packed = packed.reshape(replicas, slots * block_size, cols_here)
    target = (row_local - owner * owner_blocks + 1).astype(jnp.float32)
    tags = jnp.einsum("iqs,i->qs", select, target, precision=lax.Precision.HIGHEST) - 1.0
    col_tags = jnp.broadcast_to(col_local.astype(jnp.float32)[None, :], (replicas, leaf_cols))
    got_rows, got_tags, got_cols = in_one_piece((packed, tags, col_tags), "depth", 0, 0, 1)
    slot_pick = (
        got_tags[:, :, None] == lax.iota(jnp.int32, owner_blocks).astype(jnp.float32)[None, None, :]
    ).astype(jnp.float32)
    column_pick = (
        got_cols[:, :, None]
        == lax.iota(jnp.int32, anc_col_blocks).astype(jnp.float32)[None, None, :]
    ).astype(jnp.float32)
    pieces = got_rows.reshape(replicas, slots, block_size, leaf_cols, block_size)
    sectioned = jnp.einsum("psa,psxjy->paxjy", slot_pick, pieces, precision=lax.Precision.HIGHEST)
    placed = jnp.einsum("paxjy,pjb->axby", sectioned, column_pick, precision=lax.Precision.HIGHEST)
    return placed.reshape(anc_rows, anc_col_blocks * block_size)


def anc_panels(a21_anc, a12_anc, uinv_anc, linv_anc):
    factor = uinv_anc
    anc_lower = product(collect(a21_anc, "col", 1), factor)
    lower_whole = collect(anc_lower, "col", 1)
    factor = linv_anc
    anc_upper = product(factor, lax.all_gather(a12_anc, ("row", "depth"), axis=0, tiled=True))
    return (anc_lower, lower_whole, anc_upper)


def shards(
    a21_leaf,
    a12_leaf,
    uinv_leaf,
    linv_leaf,
    live,
    row_map,
    col_map,
    a22_anc,
    a21_anc,
    a12_anc,
    uinv_anc,
    linv_anc,
):
    block_size = NB
    panel_left = a21_leaf[0]
    panel_top = a12_leaf[0]
    upper_inverse = uinv_leaf[0]
    lower_inverse = linv_leaf[0]
    rows_here = panel_left.shape[0]
    cols_here = panel_top.shape[1]
    live_rows = live[0] * block_size
    row_pos = lax.axis_index("row") * rows_here + lax.iota(jnp.int32, rows_here)
    col_pos = lax.axis_index("col") * cols_here + lax.iota(jnp.int32, cols_here)
    row_keep = (row_pos < live_rows).astype(jnp.float32)
    col_keep = (col_pos < live_rows).astype(jnp.float32)
    factor = upper_inverse
    lower_part = product(lax.all_gather(panel_left, "col", axis=1, tiled=True), factor)
    leaf_lower = lower_part * row_keep[:, None]
    factor = lower_inverse
    upper_part = product(factor, lax.all_gather(panel_top, "row", axis=0, tiled=True))
    leaf_upper = upper_part * col_keep[None, :]
    upper_whole = lax.all_gather(leaf_upper, "row", axis=0, tiled=True)
    factor = upper_whole
    schur = jnp.zeros((rows_here, cols_here), jnp.float32) - product(
        lax.all_gather(leaf_lower, "col", axis=1, tiled=True), factor
    )
    own_update = combine_depth(schur, row_map, col_map, a22_anc)
    anc_lower, lower_whole, anc_upper = anc_panels(a21_anc, a12_anc, uinv_anc, linv_anc)
    factor = lower_whole
    anc_schur = a22_anc + own_update - product(factor, gather_axes(anc_upper, ("row", "depth"), 0))
    return (leaf_lower[None], leaf_upper[None], anc_lower, anc_upper, anc_schur)


def solution(mesh):
    in_specs = (
        P("depth", "row", "col"),
        P("depth", "row", "col"),
        P("depth", None, "col"),
        P("depth", "row", None),
        P("depth"),
        P("depth", "row"),
        P("depth", "col"),
        P(("row", "depth"), "col"),
        P(("row", "depth"), "col"),
        P(("row", "depth"), "col"),
        P(None, "col"),
        P(("row", "depth"), None),
    )
    out_specs = (
        P("depth", "row", "col"),
        P("depth", "row", "col"),
        P(("row", "depth"), "col"),
        P(("row", "depth"), "col"),
        P(("row", "depth"), "col"),
    )
    return jax.shard_map(shards, mesh=mesh, in_specs=in_specs, out_specs=out_specs, check_vma=False)
```

profile of v0, /device:TPU:1, one launch (start us, length us, event | category | flops | bytes accessed | tf_op | source)
XLA Modules:
  0.0 436.7 jit_solution(4254180319421357973)
XLA Ops:
  7.2 0.0 all-gather.20.cloned.1.call-start
  7.2 0.7 all-gather.20.cloned.1.call-update
  7.9 0.0 all-gather.22.cloned.1.call-start
  8.0 0.7 all-gather.22.cloned.1.call-update
  8.7 0.0 all-gather.10.cloned.1.call-start
  8.7 0.7 all-gather.10.cloned.1.call-update
  9.4 0.0 all-gather.12.cloned.1.call-start
  10.1 38.6 %all-gather.20.cloned.1.call-done = f32[1,512,2048]{2,1,0:T(8,128)} async-done(((f32[1,512,256]{2,1,0:T(8,128)}), f32[1,512,2048]{2,1,0:T(8,128)}) %all-gather.20.cloned.1.call-update) | async-done | bytes 4194320 | tf_op jit(solution)/shard_map/all_gather | solution.py:125
  48.7 6.4 %fusion.10 = f32[512,256]{1,0:T(8,128)} fusion(f32[1,2048,256]{2,1,0:T(8,128)S(1)} %copy-done, f32[1,512,2048]{2,1,0:T(8,128)} %all-gather.20.cloned.1.call-done, f32[512]{0:T(512)S(1)} %fusion.32), kind=kOutput, calls=%fused_computation.13 | convolution fusion | flops 3221356544 | bytes 6817792 | tf_op jit(solution)/shard_map/dot_general | solution.py:44
  55.1 0.0 all-gather.12.cloned.1.call-update
  55.1 0.0 all-gather.14.cloned.1.call-start
  55.2 49.4 %all-gather.22.cloned.1.call-done = f32[1,2048,512]{2,1,0:T(8,128)} async-done(((f32[1,256,512]{2,1,0:T(8,128)}), f32[1,2048,512]{2,1,0:T(8,128)}) %all-gather.22.cloned.1.call-update) | async-done | bytes 4194320 | tf_op jit(solution)/shard_map/all_gather | solution.py:128
  104.6 7.3 %fusion.15 = f32[256,512]{1,0:T(8,128)} fusion(f32[1,2048,512]{2,1,0:T(8,128)} %all-gather.22.cloned.1.call-done, f32[1,256,2048]{2,1,0:T(8,128)} %param.15, f32[512]{0:T(512)S(1)} %fusion.33), kind=kOutput, calls=%fused_computation.14 | convolution fusion | flops 3221356544 | bytes 6817792 | tf_op jit(solution)/shard_map/dot_general | solution.py:44
  112.0 0.1 copy.29
  112.1 1.5 broadcast_in_dim.16
  113.6 5.3 %all-to-all-start = ((f32[8,256,256]{1,2,0:T(8,128)}), f32[8,256,256]{1,2,0:T(8,128)S(1)}, u32[]{:S(2)}, u32[]{:S(2)}) async-start(f32[8,256,256]{1,2,0:T(8,128)} %broadcast_in_dim.16), calls=%async_computation | async-start | bytes 4194304 | tf_op jit(solution)/shard_map/all_to_all | solution.py:22
  118.9 0.1 convert_reduce_fusion
  119.0 84.1 %all-gather.10.cloned.1.call-done = f32[2048,1024]{1,0:T(8,128)} async-done(((f32[64,1024]{1,0:T(8,128)}), f32[2048,1024]{1,0:T(8,128)}) %all-gather.10.cloned.1.call-update) | async-done | bytes 8388624 | tf_op jit(solution)/shard_map/all_gather | solution.py:94
  203.1 8.2 %fusion.51 = f32[64,1024]{1,0:T(8,128)} fusion(f32[64,2048]{1,0:T(8,128)S(1)} %copy-done.3, f32[2048,1024]{1,0:T(8,128)} %all-gather.10.cloned.1.call-done), kind=kOutput, calls=%fused_computation.69 | convolution fusion | flops 1610612736 | bytes 9175040 | tf_op jit(solution)/shard_map/dot_general | solution.py:44
  211.4 0.2 all-gather.18.cloned.1.call-start
  211.6 0.1 fusion.27
  211.7 0.1 copy.37
  211.8 0.1 bitcast_add_fusion.1
  211.9 26.4 %all-gather.12.cloned.1.call-done = f32[512,2048]{1,0:T(8,128)} async-done(((f32[512,256]{1,0:T(8,128)}), f32[512,2048]{1,0:T(8,128)}) %all-gather.12.cloned.1.call-update) | async-done | bytes 4194320 | tf_op jit(solution)/shard_map/all_gather | solution.py:133
  238.3 56.4 %all-gather.14.cloned.1.call-done = f32[2048,512]{1,0:T(8,128)} async-done(((f32[256,512]{1,0:T(8,128)}), f32[2048,512]{1,0:T(8,128)}) %all-gather.14.cloned.1.call-update) | async-done | bytes 4194320 | tf_op jit(solution)/shard_map/all_gather | solution.py:130
  294.7 9.4 %convolution_subtract_fusion = f32[512,512]{1,0:T(8,128)S(1)} fusion(f32[512,2048]{1,0:T(8,128)} %all-gather.12.cloned.1.call-done, f32[2048,512]{1,0:T(8,128)} %all-gather.14.cloned.1.call-done), kind=kOutput, calls=%fused_computation.11 | convolution fusion | flops 6442713088 | bytes 9437184 | tf_op jit(solution)/shard_map/dot_general | solution.py:44
  304.0 3.6 fusion.20
  307.6 12.7 %all-gather.16.cloned.1.call-done = f32[256,1024]{1,0:T(8,128)} async-done(((f32[64,1024]{1,0:T(8,128)}), f32[256,1024]{1,0:T(8,128)}) %all-gather.16.cloned.1.call-update) | async-done | bytes 1048592 | tf_op jit(solution)/shard_map/all_gather | solution.py:39
  320.3 3.1 constant_dynamic-update-slice_fusion
  323.4 1.3 dynamic-update-slice.1
  324.7 1.4 dynamic-update-slice.2
  326.0 4.8 %copy.31 = f32[4,1,131078]{2,1,0:T(1,128)} copy(f32[4,1,131078]{2,0,1:T(4,128)} %bitcast.99) | data formatting | bytes 4194496 | tf_op jit(solution)/shard_map/all_to_all | solution.py:15
  330.9 4.5 %all-to-all-start.1 = ((f32[4,1,131078]{2,1,0:T(1,128)}), f32[4,1,131078]{2,1,0:T(1,128)}, u32[]{:S(2)}, u32[]{:S(2)}) async-start(f32[4,1,131078]{2,1,0:T(1,128)} %copy.31), calls=%async_computation.1 | async-start | bytes 4198400 | tf_op jit(solution)/shard_map/all_to_all | solution.py:15
  335.4 5.3 %fusion.50 = f32[256,256]{1,0:T(8,128)S(1)} fusion(f32[256,2048]{0,1:T(8,128)S(1)} %bitcast.100, f32[2048,256]{1,0:T(8,128)} %param.22), kind=kOutput, calls=%fused_computation.68 | convolution fusion | flops 1610612736 | bytes 4456448 | tf_op jit(solution)/shard_map/dot_general | solution.py:44
  340.7 0.1 copy.35
  340.8 18.3 %all-to-all-done.1 = f32[4,1,131078]{2,1,0:T(1,128)} async-done(((f32[4,1,131078]{2,1,0:T(1,128)}), f32[4,1,131078]{2,1,0:T(1,128)}, u32[]{:S(2)}, u32[]{:S(2)}) %all-to-all-start.1) | async-done | bytes 2097280 | tf_op jit(solution)/shard_map/all_to_all | solution.py:15
  359.1 1.5 broadcast_in_dim.20
  360.6 7.9 %all-to-all-start.2 = ((f32[8,256,256]{1,2,0:T(8,128)}), f32[8,256,256]{1,2,0:T(8,128)}, u32[]{:S(2)}, u32[]{:S(2)}) async-start(f32[8,256,256]{1,2,0:T(8,128)} %broadcast_in_dim.20), calls=%async_computation.2 | async-start | bytes 4194304 | tf_op jit(solution)/shard_map/all_to_all | solution.py:22
  368.5 2.6 copy.53
  371.2 1.5 split.14
  372.7 0.1 split.12
  372.8 3.4 reshape_reshape.7
  376.2 0.1 copy.32
  376.2 4.8 %fusion.8 = f32[4,2,128,4,128]{4,1,3,2,0:T(2,128)S(1)} fusion(f32[4,2,128,4,128]{4,3,2,1,0:T(4,128)S(1)} %reshape_reshape.7, f32[4,2]{1,0:T(4,128)S(1)} %split.13, f32[2]{0:T(128)S(1)} %iota_convert_fusion), kind=kOutput, calls=%fused_computation.9 | convolution fusion | flops 12582928 | bytes 4194344 | tf_op jit(solution)/shard_map/psa,psxjy->paxjy/dot_general | solution.py:84
  381.0 3.2 fusion.6
  384.3 10.6 %all-to-all-done.2 = f32[8,256,256]{1,2,0:T(8,128)} async-done(((f32[8,256,256]{1,2,0:T(8,128)}), f32[8,256,256]{1,2,0:T(8,128)}, u32[]{:S(2)}, u32[]{:S(2)}) %all-to-all-start.2) | async-done | bytes 2097184 | tf_op jit(solution)/shard_map/all_to_all | solution.py:22
  394.8 23.6 %all-gather.18.cloned.1.call-done = f32[2048,1024]{1,0:T(8,128)} async-done(((f32[256,1024]{1,0:T(8,128)}), f32[2048,1024]{1,0:T(8,128)}) %all-gather.18.cloned.1.call-update) | async-done | bytes 8388624 | tf_op jit(solution)/shard_map/all_gather | solution.py:39
  418.5 11.4 %convolution_subtract_fusion.1 = f32[256,1024]{1,0:T(8,128)} fusion(f32[256,2048]{0,1:T(8,128)} %bitcast.28, f32[2048,1024]{1,0:T(8,128)} %all-gather.18.cloned.1.call-done, f32[256,1024]{1,0:T(8,128)} %param.19, f32[32,8,8,128]{3,2,1,0:T(8,128)S(1)} %bitcast.103), kind=kOutput, calls=%fused_computation.12 | convolution fusion | flops 6442975232 | bytes 13631488 | tf_op jit(solution)/shard_map/dot_general | solution.py:44
  (30 shorter events, 0.2 us)
Async XLA Ops:
  7.2 41.5 %copy-start = (f32[1,2048,256]{2,1,0:T(8,128)S(1)}, f32[1,2048,256]{2,1,0:T(8,128)}, u32[]{:S(2)}) copy-start(f32[1,2048,256]{2,1,0:T(8,128)} %param.14) | copy-start | bytes 6291460
  7.2 41.5 %all-gather.20.cloned.1.call-start = ((), (), s32[]{:S(2)}) async-start(), calls=%async_computation.8 | async-start | bytes 4718592 | tf_op jit(solution)/shard_map/all_gather | solution.py:125
  7.9 96.7 %all-gather.22.cloned.1.call-start = ((), (), s32[]{:S(2)}) async-start(), calls=%async_computation.9 | async-start | bytes 4718592 | tf_op jit(solution)/shard_map/all_gather | solution.py:128
  8.7 194.5 %all-gather.10.cloned.1.call-start = ((), (), s32[]{:S(2)}) async-start(), calls=%async_computation.3 | async-start | bytes 8650752 | tf_op jit(solution)/shard_map/all_gather | solution.py:94
  9.4 228.9 %all-gather.12.cloned.1.call-start = ((), (), s32[]{:S(2)}) async-start(), calls=%async_computation.4 | async-start | bytes 4718592 | tf_op jit(solution)/shard_map/all_gather | solution.py:133
  55.1 239.5 %all-gather.14.cloned.1.call-start = ((), (), s32[]{:S(2)}) async-start(), calls=%async_computation.5 | async-start | bytes 4718592 | tf_op jit(solution)/shard_map/all_gather | solution.py:130
  55.2 56.8 %copy-start.4 = (f32[256,256]{1,0:T(8,128)S(1)}, f32[256,256]{1,0:T(8,128)}, u32[]{:S(2)}) copy-start(f32[256,256]{1,0:T(8,128)} %param.20) | copy-start | bytes 786436
  113.6 5.3 %copy-start.5 = (s32[1,4]{1,0:T(1,128)S(1)}, s32[1,4]{1,0:T(1,128)}, u32[]{:S(2)}) copy-start(s32[1,4]{1,0:T(1,128)} %param.17) | copy-start | bytes 52
  113.6 89.5 %copy-start.3 = (f32[64,2048]{1,0:T(8,128)S(1)}, f32[64,2048]{1,0:T(8,128)}, u32[]{:S(2)}) copy-start(f32[64,2048]{1,0:T(8,128)} %param.23) | copy-start | bytes 1572868
  113.6 217.2 %all-to-all-start = ((f32[8,256,256]{1,2,0:T(8,128)}), f32[8,256,256]{1,2,0:T(8,128)S(1)}, u32[]{:S(2)}, u32[]{:S(2)}) async-start(f32[8,256,256]{1,2,0:T(8,128)} %broadcast_in_dim.16), calls=%async_computation | async-start | bytes 4194304 | tf_op jit(solution)/shard_map/all_to_all | solution.py:22
  118.9 201.4 %all-gather.16.cloned.1.call-start = ((), (), s32[]{:S(2)}) async-start(), calls=%async_computation.6 | async-start | bytes 1310720 | tf_op jit(solution)/shard_map/all_gather | solution.py:39
  119.0 92.8 %copy-start.6 = (s32[1,4]{1,0:T(1,128)S(1)}, s32[1,4]{1,0:T(1,128)}, u32[]{:S(2)}) copy-start(s32[1,4]{1,0:T(1,128)} %param.18) | copy-start | bytes 52
  211.4 207.1 %all-gather.18.cloned.1.call-start = ((), (), s32[]{:S(2)}) async-start(), calls=%async_computation.7 | async-start | bytes 9437184 | tf_op jit(solution)/shard_map/all_gather | solution.py:39
  330.9 28.3 %all-to-all-start.1 = ((f32[4,1,131078]{2,1,0:T(1,128)}), f32[4,1,131078]{2,1,0:T(1,128)}, u32[]{:S(2)}, u32[]{:S(2)}) async-start(f32[4,1,131078]{2,1,0:T(1,128)} %copy.31), calls=%async_computation.1 | async-start | bytes 4198400 | tf_op jit(solution)/shard_map/all_to_all | solution.py:15
  340.7 20.0 %copy-start.2 = (f32[256,256]{1,0:T(8,128)}, f32[256,256]{1,0:T(8,128)S(1)}, u32[]{:S(2)}) copy-start(f32[256,256]{1,0:T(8,128)S(1)} %fusion.50) | copy-start | bytes 786436
  360.6 34.2 %all-to-all-start.2 = ((f32[8,256,256]{1,2,0:T(8,128)}), f32[8,256,256]{1,2,0:T(8,128)}, u32[]{:S(2)}, u32[]{:S(2)}) async-start(f32[8,256,256]{1,2,0:T(8,128)} %broadcast_in_dim.20), calls=%async_computation.2 | async-start | bytes 4194304 | tf_op jit(solution)/shard_map/all_to_all | solution.py:22
  418.5 11.4 %copy-start.1 = (f32[1,2048,256]{2,1,0:T(8,128)S(1)}, f32[1,2048,256]{2,1,0:T(8,128)}, u32[]{:S(2)}) copy-start(f32[1,2048,256]{2,1,0:T(8,128)} %param.14) | copy-start | bytes 6291460
Sparse Core Ops, SparseCore 0:
  9.8 38.8 all-gather.19
  50.5 54.1 all-gather.21
  107.2 95.8 all-gather.9
  205.4 32.8 all-gather.11
  240.5 54.1 all-gather.13
  296.9 23.3 all-gather.15
  322.0 96.3 all-gather.17
where the time goes:
time: 437 us
  waiting for transfers between devices  322 us (74%)
  matrix products  59.7 us (14%)
  local copies, waits for them, and re-layouts  21.7 us (5%)
  starting transfers between devices  18.1 us (4%)
  between operations  14.9 us (3%)
    all_gather x1, waiting for transfers between devices, anc_panels(): lax.all_gather(a12_anc, ('row', 'depth'), axis=0, tiled=True)  84.1 us
    all_gather x1, waiting for transfers between devices, shards(): upper_whole = lax.all_gather(leaf_upper, 'row', axis=0, tiled=True)  56.4 us
    all_gather x1, waiting for transfers between devices, shards(): lax.all_gather(panel_top, 'row', axis=0, tiled=True)  49.4 us
    dot_general x6, matrix products, product(): jnp.dot(left, right, precision=lax.Precision.HIGHEST, preferred_element_t...  48 us
    all_gather x1, waiting for transfers between devices, shards(): lax.all_gather(panel_left, 'col', axis=1, tiled=True)  38.6 us
    all_gather x2, waiting for transfers between devices, gather_axes(): out = lax.all_gather(out, axes[number], axis=dim, tiled=True)  36.3 us
    all_gather x1, waiting for transfers between devices, shards(): lax.all_gather(leaf_lower, 'col', axis=1, tiled=True)  26.4 us
    all_to_all x1, waiting for transfers between devices, in_one_piece(): lax.all_to_all(both, axis, split_axis=split_dim, concat_axis=concat_dim,...  18.3 us
  transfers between devices with their start and end apart: 10, of which 9 were waited for; matrix products, arithmetic and copies ran while one was open for 16% of the time, Pallas kernels for 0%

commit v1 on v0

--- a/solution.py
+++ b/solution.py
@@ -5,6 +5,11 @@
 from jax.sharding import PartitionSpec as P
 
 NB = 128
+
+
+def gather_from_all(value, axis, dim):
+    copies = jnp.concatenate([value] * lax.axis_size(axis), axis=dim)
+    return lax.all_to_all(copies, axis, dim, dim, tiled=True)
 
 
 def in_one_piece(arrays, axis, split_dim, concat_dim, along):
@@ -91,7 +96,7 @@
     anc_lower = product(collect(a21_anc, "col", 1), factor)
     lower_whole = collect(anc_lower, "col", 1)
     factor = linv_anc
-    anc_upper = product(factor, lax.all_gather(a12_anc, ("row", "depth"), axis=0, tiled=True))
+    anc_upper = product(factor, gather_from_all(a12_anc, ("row", "depth"), 0))
     return (anc_lower, lower_whole, anc_upper)
 
 

time: 437 us -> 481 us (1.10); the launches traced: 437 us -> 472 us
  local copies, waits for them, and re-layouts: 21.7 us -> 37 us
  starting transfers between devices: 18.1 us -> 31.9 us
    all_gather x1 -> x0, waiting for transfers between devices: 84.1 us -> none  [anc_panels(): lax.all_gather(a12_anc, ('row', 'depth'), axis=0, tiled=True)]
    all_to_all x0 -> x1, waiting for transfers between devices: none -> 83 us  [gather_from_all(): return lax.all_to_all(copies, axis, dim, dim, tiled=True)]
    all_gather x1, waiting for transfers between devices: 56.4 us -> 2.01 us  [shards(): upper_whole = lax.all_gather(leaf_upper, 'row', axis=0, tiled=True)]
    all_gather x1, waiting for transfers between devices: 49.4 us -> 95.9 us  [shards(): lax.all_gather(panel_top, 'row', axis=0, tiled=True)]
    unnamed x18 -> x53, local copies, waits for them, and re-layouts: 7.18 us -> 24.2 us
    all_to_all x0 -> x1, starting transfers between devices: none -> 12 us  [gather_from_all(): return lax.all_to_all(copies, axis, dim, dim, tiled=True)]
    all_gather x1, waiting for transfers between devices: 26.4 us -> 35.1 us  [shards(): lax.all_gather(leaf_lower, 'col', axis=1, tiled=True)]
  transfers between devices with their start and end apart: 10 -> 10, of which waited for: 9 -> 9; matrix products, arithmetic and copies ran while one was open for 16% -> 18% of each run, Pallas kernels for 0% -> 0%
where the time goes in v1:
time: 481 us; the launch traced here: 472 us
  waiting for transfers between devices  325 us (68%)
  matrix products  62 us (13%)
  local copies, waits for them, and re-layouts  37 us (8%)
  starting transfers between devices  31.9 us (7%)
  between operations  15.5 us (3%)
    all_gather x1, waiting for transfers between devices, shards(): lax.all_gather(panel_top, 'row', axis=0, tiled=True)  95.9 us
    all_to_all x1, waiting for transfers between devices, gather_from_all(): return lax.all_to_all(copies, axis, dim, dim, tiled=True)  83 us
    dot_general x6, matrix products, product(): jnp.dot(left, right, precision=lax.Precision.HIGHEST, preferred_element_t...  48.4 us
    all_gather x2, waiting for transfers between devices, gather_axes(): out = lax.all_gather(out, axes[number], axis=dim, tiled=True)  40.4 us
    all_gather x1, waiting for transfers between devices, shards(): lax.all_gather(panel_left, 'col', axis=1, tiled=True)  38.7 us
    all_gather x1, waiting for transfers between devices, shards(): lax.all_gather(leaf_lower, 'col', axis=1, tiled=True)  35.1 us
    unnamed x53, local copies, waits for them, and re-layouts  24.2 us
    all_to_all x1, waiting for transfers between devices, in_one_piece(): lax.all_to_all(both, axis, split_axis=split_dim, concat_axis=concat_dim,...  18.3 us
  transfers between devices with their start and end apart: 10, of which 9 were waited for; matrix products, arithmetic and copies ran while one was open for 18% of the time, Pallas kernels for 0%

profile of v1, /device:TPU:1, one launch (start us, length us, event | category | flops | bytes accessed | tf_op | source)
XLA Modules:
  0.0 471.6 jit_solution(13604882796122553320)
XLA Ops:
  7.2 0.7 all-gather.19.cloned.1.call-update
  8.0 0.7 all-gather.17.cloned.1.call-update
  8.7 1.0 constant_dynamic-update-slice_fusion.31
  9.7 1.0 constant_dynamic-update-slice_fusion.30
  10.6 1.0 constant_dynamic-update-slice_fusion.29
  11.6 1.0 constant_dynamic-update-slice_fusion.28
  12.6 1.0 constant_dynamic-update-slice_fusion.27
  13.5 1.0 constant_dynamic-update-slice_fusion.26
  14.5 1.0 constant_dynamic-update-slice_fusion.25
  15.5 1.0 constant_dynamic-update-slice_fusion.24
  16.5 1.0 constant_dynamic-update-slice_fusion.23
  17.4 1.0 constant_dynamic-update-slice_fusion.22
  18.4 1.0 constant_dynamic-update-slice_fusion.21
  19.4 1.0 constant_dynamic-update-slice_fusion.20
  20.4 1.0 constant_dynamic-update-slice_fusion.19
  21.3 1.0 constant_dynamic-update-slice_fusion.18
  22.8 3.2 copy-done.3
  26.1 12.0 %all-to-all-start.1 = ((f32[32,64,1024]{2,1,0:T(8,128)}), f32[32,64,1024]{2,1,0:T(8,128)}, u32[]{:S(2)}, u32[]{:S(2)}) async-start(f32[32,64,1024]{2,1,0:T(8,128)} %bitcast.100), calls=%async_computation.1 | async-start | bytes 16777216 | tf_op jit(solution)/shard_map/all_to_all | solution.py:12
  38.8 95.9 %all-gather.19.cloned.1.call-done = f32[1,2048,512]{2,1,0:T(8,128)} async-done(((f32[1,256,512]{2,1,0:T(8,128)}), f32[1,2048,512]{2,1,0:T(8,128)}) %all-gather.19.cloned.1.call-update) | async-done | bytes 4194320 | tf_op jit(solution)/shard_map/all_gather | solution.py:133
  134.7 6.7 %fusion.15 = f32[256,512]{1,0:T(8,128)} fusion(f32[1,2048,512]{2,1,0:T(8,128)} %all-gather.19.cloned.1.call-done, f32[1,256,2048]{2,1,0:T(8,128)S(1)} %copy-done, f32[512]{0:T(512)S(1)} %fusion.33), kind=kOutput, calls=%fused_computation.14 | convolution fusion | flops 3221356544 | bytes 6817792 | tf_op jit(solution)/shard_map/dot_general | solution.py:49
  141.5 38.7 %all-gather.17.cloned.1.call-done = f32[1,512,2048]{2,1,0:T(8,128)} async-done(((f32[1,512,256]{2,1,0:T(8,128)}), f32[1,512,2048]{2,1,0:T(8,128)}) %all-gather.17.cloned.1.call-update) | async-done | bytes 4194320 | tf_op jit(solution)/shard_map/all_gather | solution.py:130
  180.2 7.1 %fusion.10 = f32[512,256]{1,0:T(8,128)} fusion(f32[1,2048,256]{2,1,0:T(8,128)} %param.14, f32[1,512,2048]{2,1,0:T(8,128)} %all-gather.17.cloned.1.call-done, f32[512]{0:T(512)S(1)} %fusion.32), kind=kOutput, calls=%fused_computation.13 | convolution fusion | flops 3221356544 | bytes 6817792 | tf_op jit(solution)/shard_map/dot_general | solution.py:49
  187.6 83.0 %all-to-all-done.1 = f32[32,64,1024]{2,1,0:T(8,128)} async-done(((f32[32,64,1024]{2,1,0:T(8,128)}), f32[32,64,1024]{2,1,0:T(8,128)}, u32[]{:S(2)}, u32[]{:S(2)}) %all-to-all-start.1) | async-done | bytes 8388640 | tf_op jit(solution)/shard_map/all_to_all | solution.py:12
  270.6 1.5 broadcast_in_dim.16
  272.1 6.6 %all-to-all-start = ((f32[8,256,256]{1,2,0:T(8,128)}), f32[8,256,256]{1,2,0:T(8,128)S(1)}, u32[]{:S(2)}, u32[]{:S(2)}) async-start(f32[8,256,256]{1,2,0:T(8,128)} %broadcast_in_dim.16), calls=%async_computation | async-start | bytes 4194304 | tf_op jit(solution)/shard_map/all_to_all | solution.py:27
  278.7 8.5 %convolution_bitcast_fusion = f32[64,1024]{1,0:T(8,128)} fusion(f32[2048,1024]{1,0:T(8,128)} %bitcast.10, f32[64,2048]{1,0:T(8,128)S(1)} %copy-done.5), kind=kOutput, calls=%fused_computation.15 | convolution fusion | flops 1610612736 | bytes 9175040 | tf_op jit(solution)/shard_map/dot_general | solution.py:49
  287.2 0.5 all-gather.15.cloned.1.call-start
  288.0 2.0 all-gather.11.cloned.1.call-done
  290.0 35.1 %all-gather.9.cloned.1.call-done = f32[512,2048]{1,0:T(8,128)} async-done(((f32[512,256]{1,0:T(8,128)}), f32[512,2048]{1,0:T(8,128)}) %all-gather.9.cloned.1.call-update) | async-done | bytes 4194320 | tf_op jit(solution)/shard_map/all_gather | solution.py:138
  325.2 9.3 %convolution_subtract_fusion = f32[512,512]{1,0:T(8,128)S(1)} fusion(f32[512,2048]{1,0:T(8,128)} %all-gather.9.cloned.1.call-done, f32[2048,512]{1,0:T(8,128)} %all-gather.11.cloned.1.call-done), kind=kOutput, calls=%fused_computation.11 | convolution fusion | flops 6442713088 | bytes 9437184 | tf_op jit(solution)/shard_map/dot_general | solution.py:49
  334.5 3.6 fusion.20
  338.1 16.9 %all-gather.13.cloned.1.call-done = f32[256,1024]{1,0:T(8,128)} async-done(((f32[64,1024]{1,0:T(8,128)}), f32[256,1024]{1,0:T(8,128)}) %all-gather.13.cloned.1.call-update) | async-done | bytes 1048592 | tf_op jit(solution)/shard_map/all_gather | solution.py:44
  355.0 3.1 constant_dynamic-update-slice_fusion.32
  358.1 1.2 dynamic-update-slice.1
  359.3 1.2 dynamic-update-slice.2
  360.5 4.8 %copy.31 = f32[4,1,131078]{2,1,0:T(1,128)} copy(f32[4,1,131078]{2,0,1:T(4,128)} %bitcast.104) | data formatting | bytes 4194496 | tf_op jit(solution)/shard_map/all_to_all | solution.py:20
  365.3 4.5 all-to-all-start.2
  369.9 5.3 %fusion.50 = f32[256,256]{1,0:T(8,128)S(1)} fusion(f32[256,2048]{0,1:T(8,128)S(1)} %bitcast.105, f32[2048,256]{1,0:T(8,128)} %param.22), kind=kOutput, calls=%fused_computation.101 | convolution fusion | flops 1610612736 | bytes 4456448 | tf_op jit(solution)/shard_map/dot_general | solution.py:49
  375.3 18.3 %all-to-all-done.2 = f32[4,1,131078]{2,1,0:T(1,128)} async-done(((f32[4,1,131078]{2,1,0:T(1,128)}), f32[4,1,131078]{2,1,0:T(1,128)}, u32[]{:S(2)}, u32[]{:S(2)}) %all-to-all-start.2) | async-done | bytes 2097280 | tf_op jit(solution)/shard_map/all_to_all | solution.py:20
  393.6 1.5 broadcast_in_dim.20
  395.1 8.1 %all-to-all-start.3 = ((f32[8,256,256]{1,2,0:T(8,128)}), f32[8,256,256]{1,2,0:T(8,128)}, u32[]{:S(2)}, u32[]{:S(2)}) async-start(f32[8,256,256]{1,2,0:T(8,128)} %broadcast_in_dim.20), calls=%async_computation.3 | async-start | bytes 4194304 | tf_op jit(solution)/shard_map/all_to_all | solution.py:27
  403.3 2.6 copy.53
  406.1 3.2 reshape_reshape.7
  409.4 6.7 %fusion.8 = f32[4,2,128,4,128]{4,1,3,2,0:T(2,128)S(1)} fusion(f32[4,2,128,4,128]{4,3,2,1,0:T(4,128)} %reshape_reshape.7, f32[4,2]{1,0:T(4,128)S(1)} %split.13, f32[2]{0:T(128)S(1)} %iota_convert_fusion), kind=kOutput, calls=%fused_computation.9 | convolution fusion | flops 12582928 | bytes 4194344 | tf_op jit(solution)/shard_map/psa,psxjy->paxjy/dot_general | solution.py:89
  416.1 3.2 fusion.6
  419.4 10.1 %all-to-all-done.3 = f32[8,256,256]{1,2,0:T(8,128)} async-done(((f32[8,256,256]{1,2,0:T(8,128)}), f32[8,256,256]{1,2,0:T(8,128)}, u32[]{:S(2)}, u32[]{:S(2)}) %all-to-all-start.3) | async-done | bytes 2097184 | tf_op jit(solution)/shard_map/all_to_all | solution.py:27
  429.5 23.6 %all-gather.15.cloned.1.call-done = f32[2048,1024]{1,0:T(8,128)} async-done(((f32[256,1024]{1,0:T(8,128)}), f32[2048,1024]{1,0:T(8,128)}) %all-gather.15.cloned.1.call-update) | async-done | bytes 8388624 | tf_op jit(solution)/shard_map/all_gather | solution.py:44
  453.0 11.5 %convolution_subtract_fusion.1 = f32[256,1024]{1,0:T(8,128)} fusion(f32[256,2048]{0,1:T(8,128)} %bitcast.31, f32[2048,1024]{1,0:T(8,128)} %all-gather.15.cloned.1.call-done, f32[256,1024]{1,0:T(8,128)} %param.19, f32[32,8,8,128]{3,2,1,0:T(8,128)S(1)} %bitcast.108), kind=kOutput, calls=%fused_computation.12 | convolution fusion | flops 6442975232 | bytes 13631488 | tf_op jit(solution)/shard_map/dot_general | solution.py:49
  (65 shorter events, 1.6 us)
Async XLA Ops:
  7.2 127.6 %copy-start = (f32[1,256,2048]{2,1,0:T(8,128)S(1)}, f32[1,256,2048]{2,1,0:T(8,128)}, u32[]{:S(2)}) copy-start(f32[1,256,2048]{2,1,0:T(8,128)} %param.15) | copy-start | bytes 6291460
  7.2 15.1 %copy-start.2 = (f32[64,1024]{1,0:T(8,128)S(1)}, f32[64,1024]{1,0:T(8,128)}, u32[]{:S(2)}) copy-start(f32[64,1024]{1,0:T(8,128)} %param.21) | copy-start | bytes 786436
  7.2 127.5 %all-gather.19.cloned.1.call-start = ((), (), s32[]{:S(2)}) async-start(), calls=%async_computation.9 | async-start | bytes 4718592 | tf_op jit(solution)/shard_map/all_gather | solution.py:133
  7.9 172.3 %all-gather.17.cloned.1.call-start = ((), (), s32[]{:S(2)}) async-start(), calls=%async_computation.8 | async-start | bytes 4718592 | tf_op jit(solution)/shard_map/all_gather | solution.py:130
  22.8 3.2 copy-start.3
  26.1 244.5 %all-to-all-start.1 = ((f32[32,64,1024]{2,1,0:T(8,128)}), f32[32,64,1024]{2,1,0:T(8,128)}, u32[]{:S(2)}, u32[]{:S(2)}) async-start(f32[32,64,1024]{2,1,0:T(8,128)} %bitcast.100), calls=%async_computation.1 | async-start | bytes 16777216 | tf_op jit(solution)/shard_map/all_to_all | solution.py:12
  38.0 149.3 %copy-start.6 = (f32[256,256]{1,0:T(8,128)S(1)}, f32[256,256]{1,0:T(8,128)}, u32[]{:S(2)}) copy-start(f32[256,256]{1,0:T(8,128)} %param.20) | copy-start | bytes 786436
  38.1 149.4 %copy-start.7 = (s32[1,4]{1,0:T(1,128)S(1)}, s32[1,4]{1,0:T(1,128)}, u32[]{:S(2)}) copy-start(s32[1,4]{1,0:T(1,128)} %param.17) | copy-start | bytes 52
  38.1 252.0 %all-gather.11.cloned.1.call-start = ((), (), s32[]{:S(2)}) async-start(), calls=%async_computation.5 | async-start | bytes 4718592 | tf_op jit(solution)/shard_map/all_gather | solution.py:135
  141.4 137.3 %copy-start.5 = (f32[64,2048]{1,0:T(8,128)S(1)}, f32[64,2048]{1,0:T(8,128)}, u32[]{:S(2)}) copy-start(f32[64,2048]{1,0:T(8,128)} %param.23) | copy-start | bytes 1572868
  141.4 183.8 %all-gather.9.cloned.1.call-start = ((), (), s32[]{:S(2)}) async-start(), calls=%async_computation.4 | async-start | bytes 4718592 | tf_op jit(solution)/shard_map/all_gather | solution.py:138
  187.3 100.7 %copy-start.8 = (s32[1,4]{1,0:T(1,128)S(1)}, s32[1,4]{1,0:T(1,128)}, u32[]{:S(2)}) copy-start(s32[1,4]{1,0:T(1,128)} %param.18) | copy-start | bytes 52
  272.1 93.3 %all-to-all-start = ((f32[8,256,256]{1,2,0:T(8,128)}), f32[8,256,256]{1,2,0:T(8,128)S(1)}, u32[]{:S(2)}, u32[]{:S(2)}) async-start(f32[8,256,256]{1,2,0:T(8,128)} %broadcast_in_dim.16), calls=%async_computation | async-start | bytes 4194304 | tf_op jit(solution)/shard_map/all_to_all | solution.py:27
  278.7 76.3 %all-gather.13.cloned.1.call-start = ((), (), s32[]{:S(2)}) async-start(), calls=%async_computation.6 | async-start | bytes 1310720 | tf_op jit(solution)/shard_map/all_gather | solution.py:44
  287.2 165.8 %all-gather.15.cloned.1.call-start = ((), (), s32[]{:S(2)}) async-start(), calls=%async_computation.7 | async-start | bytes 9437184 | tf_op jit(solution)/shard_map/all_gather | solution.py:44
  365.3 28.3 %all-to-all-start.2 = ((f32[4,1,131078]{2,1,0:T(1,128)}), f32[4,1,131078]{2,1,0:T(1,128)}, u32[]{:S(2)}, u32[]{:S(2)}) async-start(f32[4,1,131078]{2,1,0:T(1,128)} %copy.31), calls=%async_computation.2 | async-start | bytes 4198400 | tf_op jit(solution)/shard_map/all_to_all | solution.py:20
  375.1 34.2 %copy-start.4 = (f32[256,256]{1,0:T(8,128)}, f32[256,256]{1,0:T(8,128)S(1)}, u32[]{:S(2)}) copy-start(f32[256,256]{1,0:T(8,128)S(1)} %fusion.50) | copy-start | bytes 786436
  395.1 34.4 %all-to-all-start.3 = ((f32[8,256,256]{1,2,0:T(8,128)}), f32[8,256,256]{1,2,0:T(8,128)}, u32[]{:S(2)}, u32[]{:S(2)}) async-start(f32[8,256,256]{1,2,0:T(8,128)} %broadcast_in_dim.20), calls=%async_computation.3 | async-start | bytes 4194304 | tf_op jit(solution)/shard_map/all_to_all | solution.py:27
  409.4 55.2 %copy-start.1 = (f32[1,256,2048]{2,1,0:T(8,128)S(1)}, f32[1,256,2048]{2,1,0:T(8,128)}, u32[]{:S(2)}) copy-start(f32[1,256,2048]{2,1,0:T(8,128)} %param.15) | copy-start | bytes 6291460
Sparse Core Ops, SparseCore 0:
  9.8 124.9 all-gather.18
  136.6 43.5 all-gather.16
  182.6 107.4 all-gather.10
  292.3 32.8 all-gather.8
  327.4 27.5 all-gather.12
  356.6 96.3 all-gather.14
